TPU v7x, 256 devices: a 2x2x32 block of a 4x8x32 slice. The times are simulated.
256 devices in a mesh: grp: 4 (over y, x), row: 64 (over z, core).
Axes of the slice: x: 2, y: 2, z: 32, core: 2. Of those that a mesh axis runs over, the one named last changes fastest.
The devices are a block of a 4x8x32 slice.
Arguments:
- prior_basis: float32 [262144, 512], P(('grp', 'row')), parts along dimension 0, may hold values from -1 to 1, as said below
- samples: float32 [4, 262144, 64], P(None, ('grp', 'row')), parts along dimension 1, may hold values from -8 to 8
Outputs:
- new_basis: float32 [262144, 256], P(('grp', 'row')), parts along dimension 0
- leaf_estimates: float32 [4, 1024], P(None, ('grp', 'row')), parts along dimension 1
There are 4 independent parts, one for each index of `grp`. A program takes and returns all parts, laid end to end along the dimension named above; each array names one. Nothing has to cross between parts.
Inputs may be any that keep to these rules, and one draw needn't show every extreme that they name: The columns of prior_basis are orthonormal to float32 rounding.
All inputs are finite; a program needn't handle non-finite values.
Results may differ from a plain program's by a relative error of at most 0.0003.
Values sent between devices are 32-bit elements; how exact they have to be, the bound alone decides.
No kernel may reach another device: no remote copies, remote signals or barrier semaphores. Data moves between devices by JAX's collectives and lax.ppermute only.
A program may use at most 64 MiB of HBM per device.

v0:
```python
import functools
import jax
import jax.numpy as jnp
from jax import lax
from jax.sharding import Mesh
from jax.sharding import PartitionSpec as P

LEAF = 256
ROW = ("row_0", "row_1")
GRP_ROW = ("grp", "row_0", "row_1")


def over_axes(array, axes):
    return functools.reduce(lax.psum, axes, array)


def local(prior_basis, samples):
    highest = lax.Precision.HIGHEST
    rounds, local_rows, columns = samples.shape
    total_leaves = local_rows // LEAF * lax.axis_size(ROW)

    def energy_terms(block):
        return jnp.dot(block.T, block, precision=highest)

    prior_terms = jnp.einsum("nk,rns->rks", prior_basis, samples, precision=highest)
    stat_terms = jnp.stack([energy_terms(samples[number]) for number in range(rounds)])
    prior_all, stat_all = lax.psum((prior_terms, stat_terms), ROW)
    new_cols = []
    estimates = []
    for number in range(rounds):
        sample_block = samples[number]
        c_added = None
        if new_cols:
            added = jnp.concatenate(new_cols, axis=1)
        c_prior = prior_all[number]
        stat = stat_all[number]
        if new_cols:
            c_added = over_axes(jnp.dot(added.T, sample_block, precision=highest), ROW)
        remainder = sample_block - jnp.dot(prior_basis, c_prior, precision=highest)
        if new_cols:
            remainder = remainder - jnp.dot(added, c_added, precision=highest)
        gram = stat - jnp.dot(c_prior.T, c_prior, precision=highest)
        if new_cols:
            gram = gram - jnp.dot(c_added.T, c_added, precision=highest)
        energy = jnp.trace(stat)
        factor = jnp.linalg.cholesky(gram)
        fresh_cols = jax.scipy.linalg.solve_triangular(factor, remainder.T, lower=True).T
        leaf_energy = jnp.sum(
            (remainder * remainder).reshape(local_rows // LEAF, LEAF, columns), axis=(1, 2)
        )
        estimates.append(jnp.sqrt(total_leaves * leaf_energy / energy))
        new_cols.append(fresh_cols)
    return (jnp.concatenate(new_cols, axis=1), jnp.stack(estimates))


def solution(mesh):
    split = Mesh(mesh.devices.reshape(mesh.shape["grp"], 32, 2), ("grp", "row_0", "row_1"))
    in_specs = (P(GRP_ROW, None), P(None, GRP_ROW, None))
    out_specs = (P(GRP_ROW, None), P(None, GRP_ROW))
    return jax.shard_map(local, mesh=split, in_specs=in_specs, out_specs=out_specs, check_vma=False)
```

profile of v0, /device:TPU:37, one launch (start us, length us, event | category | flops | bytes accessed | tf_op | source)
XLA Modules:
  0.0 842.6 jit_solution(9579060003339560665)
XLA Ops:
  7.3 1.5 convolution_bitcast_fusion.8
  8.8 1.4 convolution_bitcast_fusion.9
  10.2 1.4 convolution_bitcast_fusion.10
  11.6 1.4 convolution_bitcast_fusion.7
  13.0 4.0 fusion.2
  17.8 400.5 %all-reduce.3.cloned.1.call-done = (f32[4,512,64]{1,2,0:T(8,128)}, f32[4,64,64]{1,2,0:T(8,128)}) async-done(((f32[4,512,64]{1,2,0:T(8,128)}, f32[4,64,64]{1,2,0:T(8,128)}), (f32[4,512,64]{1,2,0:T(8,128)}, f32[4,64,64]{1,2,0:T(8,128)})) %all-reduce.3.cloned.1.call-update) | async-done | bytes 589840 | tf_op jit(solution)/shard_map/psum | solution.py:27
  418.3 1.6 select_reduce_fusion.7
  419.8 1.2 convolution_subtract_fusion.9
  421.1 1.2 convolution_subtract_fusion.4
  422.3 1.2 convolution_subtract_fusion.6
  423.6 1.8 convolution_subtract_fusion.8
  425.4 3.7 fusion.5
  429.2 2.8 fusion.6
  432.0 2.8 fusion.7
  434.8 2.8 multiply_reduce_fusion.3
  437.8 5.8 cholesky.74
  444.3 0.7 fusion.31
  444.9 4.9 custom-call.8
  449.9 1.6 fusion.14
  451.8 78.4 %psum.58 = f32[64,64]{1,0:T(8,128)S(1)} all-reduce(f32[64,64]{1,0:T(8,128)S(1)} %fusion.20), channel_id=1, replica_groups=mesh['grp'=4,'row_0'=32,'row_1'=2] {'row_0'}, use_global_device_ids=true, to_apply=%region_4.7 | all-reduce | flops 4096 | bytes 32768 | tf_op jit(solution)/shard_map/psum | solution.py:14
  530.2 31.0 %psum.59 = f32[64,64]{1,0:T(8,128)S(1)} all-reduce(f32[64,64]{1,0:T(8,128)S(1)} %psum.58), channel_id=1, replica_groups=mesh['grp'=4,'row_0'=32,'row_1'=2] {'row_1'}, use_global_device_ids=true, to_apply=%region_5.8 | all-reduce | flops 4096 | bytes 32768 | tf_op jit(solution)/shard_map/psum | solution.py:14
  561.2 1.0 convolution_subtract_fusion.7
  562.2 2.1 multiply_reduce_fusion.2
  565.3 6.6 cholesky.85
  572.5 0.7 fusion.32
  573.2 4.9 custom-call.9
  578.1 1.4 convolution_bitcast_fusion.4
  579.5 0.7 copy-done.2
  580.2 0.7 fusion.10
  580.9 76.9 %psum.60 = f32[128,64]{0,1:T(8,128)S(1)} all-reduce(f32[128,64]{0,1:T(8,128)S(1)} %fusion.10), channel_id=1, replica_groups=mesh['grp'=4,'row_0'=32,'row_1'=2] {'row_0'}, use_global_device_ids=true, to_apply=%region_6.9 | all-reduce | flops 8192 | bytes 65536 | tf_op jit(solution)/shard_map/psum | solution.py:14
  657.8 31.0 %psum.61 = f32[128,64]{0,1:T(8,128)S(1)} all-reduce(f32[128,64]{0,1:T(8,128)S(1)} %psum.60), channel_id=1, replica_groups=mesh['grp'=4,'row_0'=32,'row_1'=2] {'row_1'}, use_global_device_ids=true, to_apply=%region_7.10 | all-reduce | flops 8192 | bytes 65536 | tf_op jit(solution)/shard_map/psum | solution.py:14
  689.0 2.2 multiply_reduce_fusion.1
  691.4 5.8 cholesky.96
  697.9 0.7 fusion.33
  698.5 4.9 custom-call.10
  703.4 1.4 convolution_bitcast_fusion.2
  704.8 0.7 copy-done.3
  705.5 1.8 fusion.9
  707.3 76.7 %psum.62 = f32[192,64]{0,1:T(8,128)S(1)} all-reduce(f32[192,64]{0,1:T(8,128)S(1)} %fusion.9), channel_id=1, replica_groups=mesh['grp'=4,'row_0'=32,'row_1'=2] {'row_0'}, use_global_device_ids=true, to_apply=%region_8.11 | all-reduce | flops 12288 | bytes 98304 | tf_op jit(solution)/shard_map/psum | solution.py:14
  784.0 31.4 %psum.63 = f32[192,64]{0,1:T(8,128)S(1)} all-reduce(f32[192,64]{0,1:T(8,128)S(1)} %psum.62), channel_id=1, replica_groups=mesh['grp'=4,'row_0'=32,'row_1'=2] {'row_1'}, use_global_device_ids=true, to_apply=%region_9.12 | all-reduce | flops 12288 | bytes 98304 | tf_op jit(solution)/shard_map/psum | solution.py:14
  815.6 1.7 multiply_reduce_fusion
  817.6 5.8 cholesky.107
  824.2 0.7 fusion.34
  824.8 4.9 custom-call.11
  830.1 1.1 pad_maximum_fusion
  831.3 1.3 copy.35
  832.6 1.3 sqrt_bitcast_fusion.2
  833.9 1.3 sqrt_bitcast_fusion
  (40 shorter events, 6.7 us)
Async XLA Ops:
  7.2 5.8 copy-start
  7.2 411.1 %all-reduce.3.cloned.1.call-start = ((), (), s32[]{:S(2)}) async-start(), calls=%async_computation | async-start | bytes 1310720 | tf_op jit(solution)/shard_map/psum | solution.py:27
  13.0 412.4 %copy-start.1 = (f32[4,1024,64]{1,2,0:T(8,128)S(1)}, f32[4,1024,64]{1,2,0:T(8,128)}, u32[]{:S(2)}) copy-start(f32[4,1024,64]{1,2,0:T(8,128)} %param.6) | copy-start | bytes 3145732
  418.3 10.9 %copy-start.4 = (f32[4,512,64]{1,2,0:T(8,128)S(1)}, f32[4,512,64]{1,2,0:T(8,128)}, u32[]{:S(2)}) copy-start(f32[4,512,64]{1,2,0:T(8,128)} %get-tuple-element.12) | copy-start | bytes 1572868
  579.5 0.7 copy-start.2
  704.8 0.7 copy-start.3
Sparse Core Ops, SparseCore 0:
  17.9 400.3 all-reduce.2
where the time goes:
time: 843 us
  waiting for transfers between devices  401 us (48%)
  blocking collectives  325 us (39%)
  other arithmetic  56.6 us (7%)
  matrix products  42.5 us (5%)
  between operations  14.4 us (2%)
    psum x1, waiting for transfers between devices, local(): prior_all, stat_all = lax.psum((prior_terms, stat_terms), ROW)  401 us
    psum x6, blocking collectives, over_axes(): return functools.reduce(lax.psum, axes, array)  325 us
    another operation x12, other arithmetic, local(): factor = jnp.linalg.cholesky(gram)  26.8 us
    another operation x8, other arithmetic, local(): jax.scipy.linalg.solve_triangular(factor, remainder.T, lower=True)  22.2 us
  transfers between devices with their start and end apart: 1, of which 1 were waited for; matrix products, arithmetic and copies ran while one was open for 0% of the time, Pallas kernels for 0%

commit v1 on v0

--- a/solution.py
+++ b/solution.py
@@ -8,6 +8,15 @@
 LEAF = 256
 ROW = ("row_0", "row_1")
 GRP_ROW = ("grp", "row_0", "row_1")
+
+
+def obtain_targets(q_in, lane_axis, axis_id):
+    for dev_i in (lane_axis, axis_id):
+        q_in = jax.lax.psum(q_in, dev_i)
+    return q_in
+
+
+unite_levels_all_by_axis = functools.partial(obtain_targets, lane_axis="row_1", axis_id="row_0")
 
 
 def over_axes(array, axes):
@@ -24,7 +33,7 @@
 
     prior_terms = jnp.einsum("nk,rns->rks", prior_basis, samples, precision=highest)
     stat_terms = jnp.stack([energy_terms(samples[number]) for number in range(rounds)])
-    prior_all, stat_all = lax.psum((prior_terms, stat_terms), ROW)
+    prior_all, stat_all = unite_levels_all_by_axis((prior_terms, stat_terms))
     new_cols = []
     estimates = []
     for number in range(rounds):

time: 843 us -> 770 us (0.913)
  waiting for transfers between devices: 401 us -> 306 us
  blocking collectives: 325 us -> 346 us
    psum x1 -> x2, waiting for transfers between devices: 401 us -> 306 us  [obtain_targets(): q_in = jax.lax.psum(q_in, dev_i)]
    psum x6, blocking collectives: 325 us -> 346 us  [over_axes(): return functools.reduce(lax.psum, axes, array)]
  transfers between devices with their start and end apart: 1 -> 2, of which waited for: 1 -> 2; matrix products, arithmetic and copies ran while one was open for 0% -> 0% of each run, Pallas kernels for 0% -> 0%
where the time goes in v1:
time: 770 us; the launch traced here: 769 us
  blocking collectives  346 us (45%)
  waiting for transfers between devices  306 us (40%)
  other arithmetic  56.6 us (7%)
  matrix products  42.2 us (5%)
  between operations  14.4 us (2%)
    psum x6, blocking collectives, over_axes(): return functools.reduce(lax.psum, axes, array)  346 us
    psum x2, waiting for transfers between devices, obtain_targets(): q_in = jax.lax.psum(q_in, dev_i)  306 us
    another operation x12, other arithmetic, local(): factor = jnp.linalg.cholesky(gram)  26.8 us
    another operation x8, other arithmetic, local(): jax.scipy.linalg.solve_triangular(factor, remainder.T, lower=True)  22.2 us
  transfers between devices with their start and end apart: 2, of which 2 were waited for; matrix products, arithmetic and copies ran while one was open for 0% of the time, Pallas kernels for 0%

profile of v1, /device:TPU:37, one launch (start us, length us, event | category | flops | bytes accessed | tf_op | source)
XLA Modules:
  0.0 768.7 jit_solution(11670359480437215078)
XLA Ops:
  7.3 1.5 convolution_bitcast_fusion.8
  8.8 1.4 convolution_bitcast_fusion.9
  10.2 1.4 convolution_bitcast_fusion.10
  11.6 1.4 convolution_bitcast_fusion.7
  13.0 3.9 fusion.2
  16.9 0.7 pad_maximum_fusion.7
  17.9 66.4 %all-reduce.7.cloned.1.call-done = (f32[4,512,64]{1,2,0:T(8,128)}, f32[4,64,64]{1,2,0:T(8,128)}) async-done(((f32[4,512,64]{1,2,0:T(8,128)}, f32[4,64,64]{1,2,0:T(8,128)}), (f32[4,512,64]{1,2,0:T(8,128)}, f32[4,64,64]{1,2,0:T(8,128)})) %all-reduce.7.cloned.1.call-update) | async-done | bytes 589840 | tf_op jit(solution)/shard_map/psum | solution.py:15
  84.3 239.5 %all-reduce.5.cloned.1.call-done = (f32[4,512,64]{1,2,0:T(8,128)}, f32[4,64,64]{1,2,0:T(8,128)}) async-done(((f32[4,512,64]{1,2,0:T(8,128)}, f32[4,64,64]{1,2,0:T(8,128)}), (f32[4,512,64]{1,2,0:T(8,128)}, f32[4,64,64]{1,2,0:T(8,128)})) %all-reduce.5.cloned.1.call-update) | async-done | bytes 589840 | tf_op jit(solution)/shard_map/psum | solution.py:15
  323.9 1.6 select_reduce_fusion.7
  325.4 1.2 convolution_subtract_fusion.9
  326.7 1.2 convolution_subtract_fusion.4
  327.9 1.2 convolution_subtract_fusion.6
  329.2 1.8 convolution_subtract_fusion.8
  331.0 3.7 fusion.5
  334.8 2.8 fusion.6
  337.6 2.8 fusion.7
  340.4 2.8 multiply_reduce_fusion.3
  343.3 5.8 cholesky.74
  349.9 0.7 fusion.31
  350.5 4.9 custom-call.8
  355.4 1.4 fusion.14
  357.2 78.0 %psum.74 = f32[64,64]{1,0:T(8,128)S(1)} all-reduce(f32[64,64]{1,0:T(8,128)S(1)} %fusion.20), channel_id=1, replica_groups=mesh['grp'=4,'row_0'=32,'row_1'=2] {'row_0'}, use_global_device_ids=true, to_apply=%region_6.9 | all-reduce | flops 4096 | bytes 32768 | tf_op jit(solution)/shard_map/psum | solution.py:23
  435.2 52.3 %psum.75 = f32[64,64]{1,0:T(8,128)S(1)} all-reduce(f32[64,64]{1,0:T(8,128)S(1)} %psum.74), channel_id=1, replica_groups=mesh['grp'=4,'row_0'=32,'row_1'=2] {'row_1'}, use_global_device_ids=true, to_apply=%region_7.10 | all-reduce | flops 4096 | bytes 32768 | tf_op jit(solution)/shard_map/psum | solution.py:23
  487.5 1.0 convolution_subtract_fusion.7
  488.5 2.1 multiply_reduce_fusion.2
  491.5 6.6 cholesky.85
  499.4 4.9 custom-call.9
  504.3 1.4 convolution_bitcast_fusion.4
  505.7 0.7 copy-done.2
  506.4 0.7 fusion.10
  507.1 76.8 %psum.76 = f32[128,64]{0,1:T(8,128)S(1)} all-reduce(f32[128,64]{0,1:T(8,128)S(1)} %fusion.10), channel_id=1, replica_groups=mesh['grp'=4,'row_0'=32,'row_1'=2] {'row_0'}, use_global_device_ids=true, to_apply=%region_8.11 | all-reduce | flops 8192 | bytes 65536 | tf_op jit(solution)/shard_map/psum | solution.py:23
  583.8 30.7 %psum.77 = f32[128,64]{0,1:T(8,128)S(1)} all-reduce(f32[128,64]{0,1:T(8,128)S(1)} %psum.76), channel_id=1, replica_groups=mesh['grp'=4,'row_0'=32,'row_1'=2] {'row_1'}, use_global_device_ids=true, to_apply=%region_9.12 | all-reduce | flops 8192 | bytes 65536 | tf_op jit(solution)/shard_map/psum | solution.py:23
  614.7 2.2 multiply_reduce_fusion.1
  617.1 5.8 cholesky.96
  624.3 4.9 custom-call.10
  629.2 1.4 convolution_bitcast_fusion.2
  630.6 0.7 copy-done.3
  631.3 1.8 fusion.9
  633.1 78.3 %psum.78 = f32[192,64]{0,1:T(8,128)S(1)} all-reduce(f32[192,64]{0,1:T(8,128)S(1)} %fusion.9), channel_id=1, replica_groups=mesh['grp'=4,'row_0'=32,'row_1'=2] {'row_0'}, use_global_device_ids=true, to_apply=%region_10.13 | all-reduce | flops 12288 | bytes 98304 | tf_op jit(solution)/shard_map/psum | solution.py:23
  711.4 30.1 %psum.79 = f32[192,64]{0,1:T(8,128)S(1)} all-reduce(f32[192,64]{0,1:T(8,128)S(1)} %psum.78), channel_id=1, replica_groups=mesh['grp'=4,'row_0'=32,'row_1'=2] {'row_1'}, use_global_device_ids=true, to_apply=%region_11.14 | all-reduce | flops 12288 | bytes 98304 | tf_op jit(solution)/shard_map/psum | solution.py:23
  741.7 1.7 multiply_reduce_fusion
  743.7 5.8 cholesky.107
  750.2 0.7 fusion.34
  750.9 4.9 custom-call.11
  756.2 1.1 pad_maximum_fusion
  757.4 1.3 copy.35
  758.7 1.3 sqrt_bitcast_fusion.2
  759.9 1.3 sqrt_bitcast_fusion
  (43 shorter events, 7.6 us)
Async XLA Ops:
  7.2 5.8 copy-start
  7.2 77.1 %all-reduce.7.cloned.1.call-start = ((), (), s32[]{:S(2)}) async-start(), calls=%async_computation.1 | async-start | bytes 1310720 | tf_op jit(solution)/shard_map/psum | solution.py:15
  16.9 314.1 %copy-start.1 = (f32[4,1024,64]{1,2,0:T(8,128)S(1)}, f32[4,1024,64]{1,2,0:T(8,128)}, u32[]{:S(2)}) copy-start(f32[4,1024,64]{1,2,0:T(8,128)} %param.6) | copy-start | bytes 3145732
  17.7 306.2 %all-reduce.5.cloned.1.call-start = ((), (), s32[]{:S(2)}) async-start(), calls=%async_computation | async-start | bytes 1310720 | tf_op jit(solution)/shard_map/psum | solution.py:15
  323.9 10.9 %copy-start.4 = (f32[4,512,64]{1,2,0:T(8,128)S(1)}, f32[4,512,64]{1,2,0:T(8,128)}, u32[]{:S(2)}) copy-start(f32[4,512,64]{1,2,0:T(8,128)} %get-tuple-element.12) | copy-start | bytes 1572868
  505.7 0.7 copy-start.2
  630.6 0.7 copy-start.3
Sparse Core Ops, SparseCore 0:
  17.8 66.4 all-reduce.6
  86.7 237.1 all-reduce.4
